TPU v7x, 32 devices: a whole 2x2x4 slice. The times are simulated.
32 devices in a mesh: lat: 16 (over z, y, core), lon: 2 (over x).
Axes of the slice: x: 2, y: 2, z: 4, core: 2. Of those that a mesh axis runs over, the one named last changes fastest.
Arguments:
- features: bfloat16 [256, 128, 512], P('lat', 'lon'), may hold values from -6 to 6
- upstream: bfloat16 [256, 128, 512], P('lat', 'lon'), may hold values from -6 to 6
- kernel: bfloat16 [4608, 512], replicated, may hold values from -0.09375 to 0.09375
Outputs:
- input_grad: bfloat16 [256, 128, 512], P('lat', 'lon')
- direction: float32 [4608, 512], P('lat')
- perturbed: float32 [4608, 512], P('lat')
All inputs are finite; a program needn't handle non-finite values.
Results may differ from a plain program's by a relative error of at most 0.0032.
Values may be sent and summed in bfloat16 or wider, within the bound.
A program may use at most 128 MiB of HBM per device.

v0:
```python
import jax
import jax.numpy as jnp
from jax import lax
from jax.sharding import PartitionSpec as P


def padded_2(block, sides, width, periodic):
    for axis, dim in sides:
        count = lax.axis_size(axis)
        forward = [(i, i + 1) for i in range(count - 1)]
        if periodic:
            forward.append((count - 1, 0))
        backward = [(target, source) for source, target in forward]
        low = lax.ppermute(
            lax.slice_in_dim(block, block.shape[dim] - width, None, axis=dim), axis, forward
        )
        high = lax.ppermute(lax.slice_in_dim(block, 0, width, axis=dim), axis, backward)
        block = jnp.concatenate([low, block, high], axis=dim)
    return block


def convolve(padded, kernel, height, breadth):
    channels = kernel.shape[1]
    total = jnp.zeros((height, breadth, channels), jnp.float32)
    for a in range(3):
        for b in range(3):
            t = 3 * a + b
            total = total + jnp.dot(
                padded[a : a + height, b : b + breadth],
                kernel[t * channels : (t + 1) * channels],
                preferred_element_type=jnp.float32,
            )
    return total


def spread(padded, kernel, height, breadth):
    channels = kernel.shape[1]
    total = jnp.zeros((height, breadth, channels), jnp.float32)
    for a in range(3):
        for b in range(3):
            t = 3 * a + b
            piece = padded[2 - a : 2 - a + height, 2 - b : 2 - b + breadth]
            total = total + lax.dot_general(
                piece,
                kernel[t * channels : (t + 1) * channels],
                (((2,), (1,)), ((), ())),
                preferred_element_type=jnp.float32,
            )
    return total


def weight_terms(padded, slope, height, breadth):
    blocks = []
    for a in range(3):
        for b in range(3):
            blocks.append(
                lax.dot_general(
                    padded[a : a + height, b : b + breadth],
                    slope,
                    (((0, 1), (0, 1)), ((), ())),
                    preferred_element_type=jnp.float32,
                )
            )
    return jnp.concatenate(blocks, axis=0)


def gated(upstream, z):
    sig = jax.nn.sigmoid(z)
    return upstream.astype(jnp.float32) * sig * (1.0 + z * (1.0 - sig))


def shards(features, upstream, kernel):
    height, breadth, channels = features.shape
    wide_cols = padded_2(features, (("lon", 1),), 1, True)
    padded_x = padded_2(wide_cols, (("lat", 0),), 1, False)
    z = convolve(padded_x, kernel, height, breadth)
    slope = gated(upstream, z).astype(jnp.bfloat16)
    slope_cols = padded_2(slope, (("lon", 1),), 1, True)
    padded_slope = padded_2(slope_cols, (("lat", 0),), 1, False)
    back = upstream.astype(jnp.float32) + spread(padded_slope, kernel, height, breadth)
    input_grad = back.astype(jnp.bfloat16)
    local_grad = weight_terms(padded_x, slope, height, breadth)
    row_block = lax.psum_scatter(local_grad, "lat", scatter_dimension=0, tiled=True)
    summed = lax.psum(row_block, "lon")
    total = lax.psum(jnp.sum(summed * summed), "lat")
    count = 9.0 * channels * channels
    direction = summed / jnp.sqrt(total / count + 1e-06)
    block_rows = summed.shape[0]
    start = lax.axis_index("lat") * block_rows
    own_kernel = lax.dynamic_slice_in_dim(kernel, start, block_rows, 0)
    perturbed = own_kernel.astype(jnp.float32) + 0.05 / jnp.sqrt(count) * direction
    return (input_grad, direction, perturbed)


def solution(mesh):
    return jax.shard_map(
        shards,
        mesh=mesh,
        in_specs=(P("lat", "lon", None), P("lat", "lon", None), P()),
        out_specs=(P("lat", "lon", None), P("lat", None), P("lat", None)),
        check_vma=False,
    )
```

profile of v0, /device:TPU:0, one launch (start us, length us, event | category | flops | bytes accessed | tf_op | source)
XLA Modules:
  0.0 243.8 jit_solution(826851262055394935)
XLA Ops:
  7.2 1.1 fusion.97
  8.3 3.0 %collective-permute-start = (bf16[16,1,512]{2,1,0:T(2,128)(2,1)S(1)}, bf16[16,1,512]{2,1,0:T(2,128)(2,1)S(1)}, u32[]{:S(2)}, u32[]{:S(2)}) collective-permute-start(bf16[16,1,512]{2,1,0:T(2,128)(2,1)S(1)} %get-tuple-element.15), channel_id=1, source_target_pairs={{0,1},{1,0},{2,3},{3,2},{4,5},{5,4},{6,7},{7,6},{8,9},{9,8},{10,11... | collective-permute-start | bytes 49160 | tf_op jit(solution)/shard_map/ppermute | solution.py:14
  11.4 0.1 collective-permute-start.1
  11.4 2.1 fusion.62
  13.5 1.8 collective-permute-done.1
  15.3 1.6 collective-permute-start.2
  16.9 1.3 collective-permute-start.3
  18.2 1.8 fusion.50
  20.0 0.7 fusion.51
  20.7 1.1 collective-permute-done.3
  21.8 0.8 maximum_maximum_fusion
  22.6 0.7 fusion.36
  23.3 0.7 fusion.39
  24.0 0.7 fusion.42
  24.7 0.7 fusion.45
  25.4 0.7 fusion.48
  26.1 0.5 copy-done.4
  26.6 1.8 fusion.1
  28.4 1.7 fusion.11
  30.1 1.7 fusion.10
  31.8 1.7 fusion.9
  33.6 1.8 fusion.8
  35.3 1.7 fusion.7
  37.1 1.8 fusion.6
  38.8 1.7 fusion.5
  40.5 1.8 fusion.4
  42.3 1.8 fusion.3
  44.3 0.6 collective-permute-start.5
  44.9 1.5 collective-permute-start.4
  46.4 1.8 fusion.60
  48.2 0.1 collective-permute-done.5
  48.3 0.5 collective-permute-done.4
  48.8 1.3 collective-permute-start.6
  50.1 4.4 %collective-permute-start.7 = (bf16[1,66,512]{2,1,0:T(8,128)(2,1)S(1)}, bf16[1,66,512]{2,1,0:T(8,128)(2,1)S(1)}, u32[]{:S(2)}, u32[]{:S(2)}) collective-permute-start(bf16[1,66,512]{2,1,0:T(8,128)(2,1)S(1)} %get-tuple-element.8), channel_id=1, source_target_pairs={{0,2},{2,4},{4,6},{6,8},{8,10},{10,12},{12,14},{14,16},{16,18},{18... | collective-permute-start | bytes 202760 | tf_op jit(solution)/shard_map/ppermute | solution.py:14
  54.5 3.3 %fusion.22 = f32[16,64,512]{2,1,0:T(8,128)} fusion(bf16[16,1,512]{2,1,0:T(2,128)(2,1)S(1)} %collective-permute-done.5, bf16[16,64,512]{2,1,0:T(8,128)(2,1)S(1)} %fusion.1, bf16[4608,512]{1,0:T(8,128)(2,1)} %param.5), kind=kOutput, calls=%fused_computation.37 | convolution fusion | flops 538968064 | bytes 3686400 | tf_op jit(solution)/shard_map/dot_general | solution.py:43
  57.9 3.1 %fusion.20 = f32[16,64,512]{2,1,0:T(8,128)} fusion(bf16[16,64,512]{2,1,0:T(8,128)(2,1)S(1)} %fusion.1, bf16[16,1,512]{2,1,0:T(2,128)(2,1)S(1)} %collective-permute-done.4, bf16[4608,512]{1,0:T(8,128)(2,1)} %param.5), kind=kOutput, calls=%fused_computation.34 | convolution fusion | flops 538968064 | bytes 3686400 | tf_op jit(solution)/shard_map/dot_general | solution.py:43
  61.0 0.8 pad_maximum_fusion.1
  61.8 3.6 %fusion.16 = f32[16,64,512]{2,1,0:T(8,128)} fusion(bf16[17,66,512]{2,1,0:T(8,128)(2,1)S(1)} %get-tuple-element.6, bf16[4608,512]{1,0:T(8,128)(2,1)} %param.5), kind=kOutput, calls=%fused_computation.29 | convolution fusion | flops 536870912 | bytes 3670016 | tf_op jit(solution)/shard_map/dot_general | solution.py:43
  65.4 3.2 %fusion.18 = f32[16,64,512]{2,1,0:T(8,128)} fusion(bf16[17,66,512]{2,1,0:T(8,128)(2,1)S(1)} %get-tuple-element.6, bf16[4608,512]{1,0:T(8,128)(2,1)} %param.5), kind=kOutput, calls=%fused_computation.31 | convolution fusion | flops 536870912 | bytes 3670016 | tf_op jit(solution)/shard_map/dot_general | solution.py:43
  68.5 3.2 %fusion.24 = f32[16,64,512]{2,1,0:T(8,128)} fusion(bf16[17,66,512]{2,1,0:T(8,128)(2,1)S(1)} %get-tuple-element.5, bf16[4608,512]{1,0:T(8,128)(2,1)} %param.5), kind=kOutput, calls=%fused_computation.39 | convolution fusion | flops 536870912 | bytes 3670016 | tf_op jit(solution)/shard_map/dot_general | solution.py:43
  71.7 86.7 %reduce-scatter.2.cloned.1.call-done = f32[288,512]{1,0:T(8,128)} async-done(((f32[4608,512]{1,0:T(8,128)}), f32[288,512]{1,0:T(8,128)}) %reduce-scatter.2.cloned.1.call-update) | async-done | bytes 589840 | tf_op jit(solution)/shard_map/reduce_scatter | solution.py:83
  158.4 3.6 %fusion.26 = f32[16,64,512]{2,1,0:T(8,128)} fusion(bf16[17,66,512]{2,1,0:T(8,128)(2,1)} %copy-done.2, bf16[4608,512]{1,0:T(8,128)(2,1)} %param.5), kind=kOutput, calls=%fused_computation.41 | convolution fusion | flops 536870912 | bytes 3670016 | tf_op jit(solution)/shard_map/dot_general | solution.py:43
  162.0 3.2 %fusion.28 = f32[16,64,512]{2,1,0:T(8,128)} fusion(bf16[17,66,512]{2,1,0:T(8,128)(2,1)S(1)} %copy-done.3, bf16[4608,512]{1,0:T(8,128)(2,1)} %param.5), kind=kOutput, calls=%fused_computation.43 | convolution fusion | flops 536870912 | bytes 3670016 | tf_op jit(solution)/shard_map/dot_general | solution.py:43
  165.2 25.2 %all-reduce.2.cloned.1.call-done = f32[288,512]{1,0:T(8,128)} async-done(((f32[288,512]{1,0:T(8,128)}), f32[288,512]{1,0:T(8,128)}) %all-reduce.2.cloned.1.call-update) | async-done | bytes 589840 | tf_op jit(solution)/shard_map/psum | solution.py:84
  190.5 1.8 multiply_reduce_fusion
  192.3 7.9 %fusion.2 = bf16[16,64,512]{2,1,0:T(8,128)(2,1)} fusion(bf16[16,64,512]{2,1,0:T(8,128)(2,1)S(1)} %copy-done.5, f32[16,64,512]{2,1,0:T(8,128)} %fusion.16, f32[16,64,512]{2,1,0:T(8,128)} %fusion.18, f32[16,64,512]{2,1,0:T(8,128)} %fusion.20, f32[16,64,512]{2,1,0:T(8,128)S(1)} %fusion.60, f32[16,64,512]{2,1,0:T(8,128)} %fusion.22, f32[16,64,512]{2,1,0:T(8,128)} %fusion.24, ...), kind=kOutput, calls=%fused_computation.4 | convolution fusion | flops 542638080 | bytes 20447232 | tf_op jit(solution)/shard_map/dot_general | solution.py:43
  200.2 33.7 %psum.15 = f32[]{:T(128)} all-reduce(f32[]{:T(128)} %multiply_reduce_fusion), channel_id=1, replica_groups=mesh['lat'=16,'lon'=2] {'lat'}, use_global_device_ids=true, to_apply=%region_3.0 | all-reduce | flops 1 | bytes 8 | tf_op jit(solution)/shard_map/psum | solution.py:85
  234.6 2.3 multiply_add_fusion
  (24 shorter events, 0.3 us)
Async XLA Ops:
  7.2 8.1 %copy-start = (bf16[16,64,512]{2,1,0:T(8,128)(2,1)S(1)}, bf16[16,64,512]{2,1,0:T(8,128)(2,1)}, u32[]{:S(2)}) copy-start(bf16[16,64,512]{2,1,0:T(8,128)(2,1)} %param.3) | copy-start | bytes 3145732
  7.2 151.2 %reduce-scatter.2.cloned.1.call-start = ((), (), s32[]{:S(2)}) async-start(), calls=%async_computation.1 | async-start | bytes 10027008 | tf_op jit(solution)/shard_map/reduce_scatter | solution.py:83
  8.3 5.2 %collective-permute-start = (bf16[16,1,512]{2,1,0:T(2,128)(2,1)S(1)}, bf16[16,1,512]{2,1,0:T(2,128)(2,1)S(1)}, u32[]{:S(2)}, u32[]{:S(2)}) collective-permute-start(bf16[16,1,512]{2,1,0:T(2,128)(2,1)S(1)} %get-tuple-element.15), channel_id=1, source_target_pairs={{0,1},{1,0},{2,3},{3,2},{4,5},{5,4},{6,7},{7,6},{8,9},{9,8},{10,11... | collective-permute-start | bytes 49160 | tf_op jit(solution)/shard_map/ppermute | solution.py:14
  11.4 3.9 %collective-permute-start.1 = (bf16[16,1,512]{2,1,0:T(2,128)(2,1)S(1)}, bf16[16,1,512]{2,1,0:T(2,128)(2,1)S(1)}, u32[]{:S(2)}, u32[]{:S(2)}) collective-permute-start(bf16[16,1,512]{2,1,0:T(2,128)(2,1)S(1)} %get-tuple-element.16), channel_id=1, source_target_pairs={{1,0},{0,1},{3,2},{2,3},{5,4},{4,5},{7,6},{6,7},{9,8},{8,9},{11,10... | collective-permute-start | bytes 49160 | tf_op jit(solution)/shard_map/ppermute | solution.py:17
  15.3 4.7 %copy-start.6 = (bf16[4608,512]{1,0:T(8,128)(2,1)S(1)}, bf16[4608,512]{1,0:T(8,128)(2,1)}, u32[]{:S(2)}) copy-start(bf16[4608,512]{1,0:T(8,128)(2,1)} %param.5) | copy-start | bytes 14155780
  15.3 5.4 %collective-permute-start.2 = (bf16[1,66,512]{2,1,0:T(8,128)(2,1)S(1)}, bf16[1,66,512]{2,1,0:T(8,128)(2,1)S(1)}, u32[]{:S(2)}, u32[]{:S(2)}) collective-permute-start(bf16[1,66,512]{2,1,0:T(8,128)(2,1)S(1)} %get-tuple-element.11), channel_id=1, source_target_pairs={{0,2},{2,4},{4,6},{6,8},{8,10},{10,12},{12,14},{14,16},{16,18},{18... | collective-permute-start | bytes 202760 | tf_op jit(solution)/shard_map/ppermute | solution.py:14
  16.9 4.9 %collective-permute-start.3 = (bf16[1,66,512]{2,1,0:T(8,128)(2,1)S(1)}, bf16[1,66,512]{2,1,0:T(8,128)(2,1)S(1)}, u32[]{:S(2)}, u32[]{:S(2)}) collective-permute-start(bf16[1,66,512]{2,1,0:T(8,128)(2,1)S(1)} %get-tuple-element.12), channel_id=1, source_target_pairs={{2,0},{4,2},{6,4},{8,6},{10,8},{12,10},{14,12},{16,14},{18,16},{20... | collective-permute-start | bytes 202760 | tf_op jit(solution)/shard_map/ppermute | solution.py:17
  25.4 1.2 copy-start.4
  44.2 146.3 %all-reduce.2.cloned.1.call-start = ((), (), s32[]{:S(2)}) async-start(), calls=%async_computation.2 | async-start | bytes 1179648 | tf_op jit(solution)/shard_map/psum | solution.py:84
  44.3 4.0 %collective-permute-start.5 = (bf16[16,1,512]{2,1,0:T(2,128)(2,1)S(1)}, bf16[16,1,512]{2,1,0:T(2,128)(2,1)S(1)}, u32[]{:S(2)}, u32[]{:S(2)}) collective-permute-start(bf16[16,1,512]{2,1,0:T(2,128)(2,1)S(1)} %get-tuple-element.14), channel_id=1, source_target_pairs={{1,0},{0,1},{3,2},{2,3},{5,4},{4,5},{7,6},{6,7},{9,8},{8,9},{11,10... | collective-permute-start | bytes 49160 | tf_op jit(solution)/shard_map/ppermute | solution.py:17
  44.9 3.9 %collective-permute-start.4 = (bf16[16,1,512]{2,1,0:T(2,128)(2,1)S(1)}, bf16[16,1,512]{2,1,0:T(2,128)(2,1)S(1)}, u32[]{:S(2)}, u32[]{:S(2)}) collective-permute-start(bf16[16,1,512]{2,1,0:T(2,128)(2,1)S(1)} %get-tuple-element.13), channel_id=1, source_target_pairs={{0,1},{1,0},{2,3},{3,2},{4,5},{5,4},{6,7},{7,6},{8,9},{9,8},{10,11... | collective-permute-start | bytes 49160 | tf_op jit(solution)/shard_map/ppermute | solution.py:14
  48.8 12.2 %collective-permute-start.6 = (bf16[1,66,512]{2,1,0:T(8,128)(2,1)S(1)}, bf16[1,66,512]{2,1,0:T(8,128)(2,1)S(1)}, u32[]{:S(2)}, u32[]{:S(2)}) collective-permute-start(bf16[1,66,512]{2,1,0:T(8,128)(2,1)S(1)} %get-tuple-element.7), channel_id=1, source_target_pairs={{2,0},{4,2},{6,4},{8,6},{10,8},{12,10},{14,12},{16,14},{18,16},{20... | collective-permute-start | bytes 202760 | tf_op jit(solution)/shard_map/ppermute | solution.py:17
  50.1 10.9 %collective-permute-start.7 = (bf16[1,66,512]{2,1,0:T(8,128)(2,1)S(1)}, bf16[1,66,512]{2,1,0:T(8,128)(2,1)S(1)}, u32[]{:S(2)}, u32[]{:S(2)}) collective-permute-start(bf16[1,66,512]{2,1,0:T(8,128)(2,1)S(1)} %get-tuple-element.8), channel_id=1, source_target_pairs={{0,2},{2,4},{4,6},{6,8},{8,10},{10,12},{12,14},{14,16},{16,18},{18... | collective-permute-start | bytes 202760 | tf_op jit(solution)/shard_map/ppermute | solution.py:14
  61.8 6.8 %copy-start.1 = (bf16[17,66,512]{2,1,0:T(8,128)(2,1)}, bf16[17,66,512]{2,1,0:T(8,128)(2,1)S(1)}, u32[]{:S(2)}) copy-start(bf16[17,66,512]{2,1,0:T(8,128)(2,1)S(1)} %get-tuple-element.6) | copy-start | bytes 3446788
  61.8 6.8 %copy-start.2 = (bf16[17,66,512]{2,1,0:T(8,128)(2,1)}, bf16[17,66,512]{2,1,0:T(8,128)(2,1)S(1)}, u32[]{:S(2)}) copy-start(bf16[17,66,512]{2,1,0:T(8,128)(2,1)S(1)} %get-tuple-element.5) | copy-start | bytes 3446788
  158.4 3.6 %copy-start.3 = (bf16[17,66,512]{2,1,0:T(8,128)(2,1)S(1)}, bf16[17,66,512]{2,1,0:T(8,128)(2,1)}, u32[]{:S(2)}) copy-start(bf16[17,66,512]{2,1,0:T(8,128)(2,1)} %copy-done.2) | copy-start | bytes 3446788
  162.0 30.3 %copy-start.5 = (bf16[16,64,512]{2,1,0:T(8,128)(2,1)S(1)}, bf16[16,64,512]{2,1,0:T(8,128)(2,1)}, u32[]{:S(2)}) copy-start(bf16[16,64,512]{2,1,0:T(8,128)(2,1)} %param.4) | copy-start | bytes 3145732
Sparse Core Ops, SparseCore 0:
  44.3 114.0 reduce-scatter.1
  160.7 29.7 all-reduce.1
where the time goes:
time: 244 us
  waiting for transfers between devices  115 us (47%)
  matrix products  58.5 us (24%)
  blocking collectives  33.7 us (14%)
  between operations  14.9 us (6%)
  starting transfers between devices  13.8 us (6%)
  other arithmetic  5.77 us (2%)
    reduce_scatter x1, waiting for transfers between devices, shards(): lax.psum_scatter(local_grad, 'lat', scatter_dimension=0, tiled=True)  86.7 us
    psum x1, blocking collectives, shards(): total = lax.psum(jnp.sum(summed * summed), 'lat')  33.7 us
    dot_general x9, matrix products, spread(): lax.dot_general(piece, kernel[t * channels:(t + 1) * channels], (((2,), (...  32.9 us
    psum x1, waiting for transfers between devices, shards(): summed = lax.psum(row_block, 'lon')  25.2 us
    dot_general x9, matrix products, weight_terms(): lax.dot_general(padded[a:a + height, b:b + breadth], slope, (((0, 1), (0,...  15.7 us
    ppermute x4, starting transfers between devices, padded_2(): lax.ppermute(lax.slice_in_dim(block, block.shape[dim] - width, None, axis...  10.5 us
    dot_general x9, matrix products, convolve(): jnp.dot(padded[a:a + height, b:b + breadth], kernel[t * channels:(t + 1)...  9.83 us
  transfers between devices with their start and end apart: 10, of which 6 were waited for; matrix products, arithmetic and copies ran while one was open for 12% of the time, Pallas kernels for 0%

commit v1 on v0

v1 whole, which is shorter than its diff:
```python
import functools

import jax
import jax.numpy as jnp
from jax import lax
from jax.experimental import pallas as pl
from jax.experimental.pallas import tpu as pltpu
from jax.sharding import PartitionSpec as P

MESH = pl.DeviceIdType.MESH


def padded_2(block, sides, width, periodic):
    for axis, dim in sides:
        count = lax.axis_size(axis)
        forward = [(i, i + 1) for i in range(count - 1)]
        if periodic:
            forward.append((count - 1, 0))
        backward = [(target, source) for source, target in forward]
        low = lax.ppermute(
            lax.slice_in_dim(block, block.shape[dim] - width, None, axis=dim), axis, forward
        )
        high = lax.ppermute(lax.slice_in_dim(block, 0, width, axis=dim), axis, backward)
        block = jnp.concatenate([low, block, high], axis=dim)
    return block


def gated(upstream, z):
    sig = jax.nn.sigmoid(z)
    return upstream.astype(jnp.float32) * sig * (1.0 + z * (1.0 - sig))


def slots_in_order(bits):
    order = [0]
    for _ in range(bits):
        order = [2 * v for v in order] + [2 * v + 1 for v in order]
    reverse = lambda v: int(format(v, "b").zfill(bits)[::-1], 2) if bits else 0
    return sorted(order, key=reverse, reverse=True)


def reduce_kernel(n_lat, n_lon, count, *refs):
    grad, own, direction, perturbed, acc, send, recv, beside, squares = refs[:9]
    send_sem, recv_sem, lon_send, lon_recv, sq_send, sq_recv = refs[9:]
    rows, channels = own.shape
    lat = lax.axis_index("lat")
    lon = lax.axis_index("lon")
    stages = n_lat.bit_length() - 1
    bit = [(lat // 2**s) % 2 for s in range(stages)]

    barrier = pltpu.get_barrier_semaphore()
    for k in range(1, n_lat):
        pl.semaphore_signal(
            barrier, inc=1, device_id={"lat": lax.rem(lat + k, n_lat)}, device_id_type=MESH
        )
    for k in range(1, n_lon):
        pl.semaphore_signal(
            barrier, inc=1, device_id={"lon": lax.rem(lon + k, n_lon)}, device_id_type=MESH
        )
    pl.semaphore_wait(barrier, n_lat + n_lon - 2)

    base = [0]
    for s in range(stages):
        base.append(base[-1] + n_lat // 2 ** (s + 1))

    def rows_of(r):
        block = lat
        for s in range(stages):
            if (r >> s) & 1:
                block = block + 2**s * (1 - 2 * bit[s])
        return pl.ds(pl.multiple_of(block * rows, 16), rows)

    def copy(s, slot):
        k = base[s] + slot
        return pltpu.make_async_remote_copy(
            src_ref=send.at[k],
            dst_ref=recv.at[k],
            send_sem=send_sem.at[k],
            recv_sem=recv_sem.at[k],
            device_id={"lat": lat + 2**s * (1 - 2 * bit[s])},
            device_id_type=MESH,
        )

    for slot in slots_in_order(stages - 1):
        send[base[0] + slot] = grad[rows_of(2 * slot + 1), :].astype(jnp.bfloat16)
        copy(0, slot).start()
    for s in range(stages):
        for slot in slots_in_order(stages - 1 - s):
            copy(s, slot).wait_recv()
            got = recv[base[s] + slot].astype(jnp.float32)
            r = slot << (s + 1)
            value = got + (grad[rows_of(r), :] if s == 0 else acc[r >> 1])
            if s + 1 == stages:
                beside[lon] = value.astype(jnp.bfloat16)
            elif slot % 2:
                send[base[s + 1] + slot // 2] = value.astype(jnp.bfloat16)
                copy(s + 1, slot // 2).start()
            else:
                acc[r >> 1] = value

    def lon_copy(k, source):
        return pltpu.make_async_remote_copy(
            src_ref=beside.at[source],
            dst_ref=beside.at[source],
            send_sem=lon_send.at[k],
            recv_sem=lon_recv.at[source],
            device_id={"lon": lax.rem(lon + k, n_lon)},
            device_id_type=MESH,
        )

    for k in range(1, n_lon):
        lon_copy(k, lon).start()
    for k in range(1, n_lon):
        lon_copy(k, lax.rem(lon + k, n_lon)).wait_recv()
    summed = beside[0].astype(jnp.float32)
    for k in range(1, n_lon):
        summed = summed + beside[k].astype(jnp.float32)
    direction[...] = summed

    square = jnp.sum((summed * summed).reshape(rows // 8, 8, channels), axis=0)
    part = square[:, :128]
    for c in range(128, channels, 128):
        part = part + square[:, c : c + 128]
    squares[lat] = part

    def square_copy(k, source):
        return pltpu.make_async_remote_copy(
            src_ref=squares.at[source],
            dst_ref=squares.at[source],
            send_sem=sq_send.at[k],
            recv_sem=sq_recv.at[source],
            device_id={"lat": lax.rem(lat + k, n_lat)},
            device_id_type=MESH,
        )

    for k in range(1, n_lat):
        square_copy(k, lat).start()
    for k in range(1, n_lat):
        square_copy(k, lax.rem(lat + k, n_lat)).wait_recv()
    total = jnp.sum(jnp.sum(squares[...], axis=0), keepdims=True)
    scaled = direction[...] / jnp.sqrt(total / count + 1e-06)
    direction[...] = scaled
    perturbed[...] = own[...].astype(jnp.float32) + 0.05 / count**0.5 * scaled

    for s in range(stages):
        for slot in range(n_lat >> (s + 1)):
            copy(s, slot).wait_send()
    for k in range(1, n_lon):
        lon_copy(k, lon).wait_send()
    for k in range(1, n_lat):
        square_copy(k, lat).wait_send()


def reduce_and_scale(grad, own, count):
    n_lat, n_lon = lax.axis_size("lat"), lax.axis_size("lon")
    rows, channels = own.shape
    block = jax.ShapeDtypeStruct((rows, channels), jnp.float32)
    vmem = pl.BlockSpec(memory_space=pltpu.VMEM)
    return pl.pallas_call(
        functools.partial(reduce_kernel, n_lat, n_lon, count),
        out_shape=(block, block),
        in_specs=[vmem, vmem],
        out_specs=(vmem, vmem),
        scratch_shapes=[
            pltpu.VMEM((n_lat // 2, rows, channels), jnp.float32),
            pltpu.VMEM((n_lat - 1, rows, channels), jnp.bfloat16),
            pltpu.VMEM((n_lat - 1, rows, channels), jnp.bfloat16),
            pltpu.VMEM((n_lon, rows, channels), jnp.bfloat16),
            pltpu.VMEM((n_lat, 8, 128), jnp.float32),
            pltpu.SemaphoreType.DMA((n_lat - 1,)),
            pltpu.SemaphoreType.DMA((n_lat - 1,)),
            pltpu.SemaphoreType.DMA((n_lon,)),
            pltpu.SemaphoreType.DMA((n_lon,)),
            pltpu.SemaphoreType.DMA((n_lat,)),
            pltpu.SemaphoreType.DMA((n_lat,)),
        ],
        compiler_params=pltpu.CompilerParams(
            collective_id=0, has_side_effects=True, vmem_limit_bytes=48 * 2**20
        ),
    )(grad, own)


def shards(features, upstream, kernel):
    height, breadth, channels = features.shape
    wide = 3 * channels
    wide_cols = padded_2(features, (("lon", 1),), 1, True)
    padded_x = padded_2(wide_cols, (("lat", 0),), 1, False)
    beside = jnp.concatenate([padded_x[:, b : b + breadth] for b in range(3)], axis=2)
    beside = beside.reshape((height + 2) * breadth, wide)
    views = [beside[a * breadth : (a + height) * breadth] for a in range(3)]
    z = sum(
        jnp.dot(views[a], kernel[a * wide : (a + 1) * wide], preferred_element_type=jnp.float32)
        for a in range(3)
    )
    slope = gated(upstream.reshape(-1, channels), z).astype(jnp.bfloat16)
    local_grad = jnp.concatenate(
        [
            lax.dot_general(
                view, slope, (((0,), (0,)), ((), ())), preferred_element_type=jnp.float32
            )
            for view in views
        ],
        axis=0,
    )
    slope = slope.reshape(height, breadth, channels)
    slope_cols = padded_2(slope, (("lon", 1),), 1, True)
    padded_slope = padded_2(slope_cols, (("lat", 0),), 1, False)
    back = lax.conv_general_dilated(
        padded_slope[None],
        kernel.reshape(3, 3, channels, channels)[::-1, ::-1],
        (1, 1),
        "VALID",
        dimension_numbers=("NHWC", "HWOI", "NHWC"),
        preferred_element_type=jnp.float32,
    )[0]
    input_grad = (upstream.astype(jnp.float32) + back).astype(jnp.bfloat16)
    count = 9.0 * channels * channels
    block_rows = kernel.shape[0] // lax.axis_size("lat")
    start = lax.axis_index("lat") * block_rows
    own_kernel = lax.dynamic_slice_in_dim(kernel, start, block_rows, 0)
    direction, perturbed = reduce_and_scale(local_grad, own_kernel, count)
    return (input_grad, direction, perturbed)


def solution(mesh):
    return jax.shard_map(
        shards,
        mesh=mesh,
        in_specs=(P("lat", "lon", None), P("lat", "lon", None), P()),
        out_specs=(P("lat", "lon", None), P("lat", None), P("lat", None)),
        check_vma=False,
    )
```

time: 244 us -> 134 us (0.55)
  waiting for transfers between devices: 115 us -> 5.53 us
  Pallas kernels: 0 us -> 66.2 us
  matrix products: 58.5 us -> 20.6 us
  blocking collectives: 33.7 us -> 0 us
  between operations: 14.9 us -> 0.92 us
  local copies, waits for them, and re-layouts: 1.7 us -> 13.9 us
  other arithmetic: 5.77 us -> 13.4 us
    reduce_scatter x1 -> x0, waiting for transfers between devices: 86.7 us -> none  [shards(): lax.psum_scatter(local_grad, 'lat', scatter_dimension=0, tiled=True)]
    pallas_call x0 -> x1, Pallas kernels: none -> 66.2 us  [reduce_and_scale(): pl.pallas_call(functools.partial(reduce_kernel, n_lat, n_lon, count), out...]
    dot_general x27 -> x6, matrix products: 58.5 us -> 14.9 us  [the longest x3 8.93 us: shards(): lax.dot_general(view, slope, (((0,), (0,)), ((), ())), preferred_element_...]
    psum x1 -> x0, blocking collectives: 33.7 us -> none  [shards(): total = lax.psum(jnp.sum(summed * summed), 'lat')]
    psum x1 -> x0, waiting for transfers between devices: 25.2 us -> none  [shards(): summed = lax.psum(row_block, 'lon')]
    concatenate x0 -> x2, other arithmetic: none -> 7.95 us  [the longest x1 7.63 us: shards(): jnp.concatenate([lax.dot_general(view, slope, (((0,), (0,)), ((), ())), p...]
    conv_general_dilated x0 -> x1, matrix products: none -> 5.67 us  [shards(): lax.conv_general_dilated(padded_slope[None], kernel.reshape(3, 3, channel...]
    unnamed x14 -> x25, local copies, waits for them, and re-layouts: 0.54 us -> 5.96 us
  transfers between devices with their start and end apart: 10 -> 8, of which waited for: 6 -> 3; matrix products, arithmetic and copies ran while one was open for 12% -> 12% of each run, Pallas kernels for 0% -> 49%
where the time goes in v1:
time: 134 us
  Pallas kernels  66.2 us (49%)
  matrix products  20.6 us (15%)
  local copies, waits for them, and re-layouts  13.9 us (10%)
  starting transfers between devices  13.6 us (10%)
  other arithmetic  13.4 us (10%)
  waiting for transfers between devices  5.53 us (4%)
    pallas_call x1, Pallas kernels, reduce_and_scale(): pl.pallas_call(functools.partial(reduce_kernel, n_lat, n_lon, count), out...  66.2 us
    ppermute x4, starting transfers between devices, padded_2(): lax.ppermute(lax.slice_in_dim(block, block.shape[dim] - width, None, axis...  9.75 us
    dot_general x3, matrix products, shards(): lax.dot_general(view, slope, (((0,), (0,)), ((), ())), preferred_element_...  8.93 us
    concatenate x1, other arithmetic, shards(): jnp.concatenate([lax.dot_general(view, slope, (((0,), (0,)), ((), ())), p...  7.63 us
    dot_general x3, matrix products, shards(): jnp.dot(views[a], kernel[a * wide:(a + 1) * wide], preferred_element_type...  6.02 us
    unnamed x25, local copies, waits for them, and re-layouts  5.96 us
    conv_general_dilated x1, matrix products, shards(): lax.conv_general_dilated(padded_slope[None], kernel.reshape(3, 3, channel...  5.67 us
    ppermute x4, waiting for transfers between devices, padded_2(): lax.ppermute(lax.slice_in_dim(block, 0, width, axis=dim), axis, backward)  5.52 us
  transfers between devices with their start and end apart: 8, of which 3 were waited for; matrix products, arithmetic and copies ran while one was open for 12% of the time, Pallas kernels for 49%

profile of v1, /device:TPU:0, one launch (start us, length us, event | category | flops | bytes accessed | tf_op | source)
XLA Modules:
  0.0 134.2 jit_solution(16113339344612301177)
XLA Ops:
  0.6 1.0 fusion.31
  1.7 3.0 %collective-permute-start = (bf16[16,1,512]{2,1,0:T(2,128)(2,1)S(1)}, bf16[16,1,512]{2,1,0:T(2,128)(2,1)S(1)}, u32[]{:S(2)}, u32[]{:S(2)}) collective-permute-start(bf16[16,1,512]{2,1,0:T(2,128)(2,1)S(1)} %get-tuple-element.22), channel_id=1, source_target_pairs={{0,1},{1,0},{2,3},{3,2},{4,5},{5,4},{6,7},{7,6},{8,9},{9,8},{10,11... | collective-permute-start | bytes 49160 | tf_op jit(solution)/shard_map/ppermute | solution.py:20
  4.7 0.1 collective-permute-start.1
  4.8 1.8 %copy_convert_fusion = f32[16,64,512]{2,0,1:T(8,128)S(1)} fusion(bf16[16,64,512]{2,1,0:T(8,128)(2,1)} %param.4), kind=kLoop, calls=%fused_computation.25 | loop fusion | flops 524288 | bytes 3145728 | tf_op jit(solution)/shard_map/convert_element_type | solution.py:215
  6.6 1.2 copy.7
  7.9 0.7 collective-permute-done.1
  8.7 1.3 collective-permute-start.2
  10.0 1.5 %collective-permute-start.3 = (bf16[1,66,512]{2,1,0:T(8,128)(2,1)S(1)}, bf16[1,66,512]{2,1,0:T(8,128)(2,1)S(1)}, u32[]{:S(2)}, u32[]{:S(2)}) collective-permute-start(bf16[1,66,512]{2,1,0:T(8,128)(2,1)S(1)} %get-tuple-element.17), channel_id=1, source_target_pairs={{2,0},{4,2},{6,4},{8,6},{10,8},{12,10},{14,12},{16,14},{18,16},{20... | collective-permute-start | bytes 202760 | tf_op jit(solution)/shard_map/ppermute | solution.py:23
  11.4 1.0 constant_dynamic-slice_fusion.refs_1_
  12.4 2.4 %collective-permute-done.3 = bf16[1,66,512]{2,1,0:T(8,128)(2,1)S(1)} collective-permute-done((bf16[1,66,512]{2,1,0:T(8,128)(2,1)S(1)}, bf16[1,66,512]{2,1,0:T(8,128)(2,1)S(1)}, u32[]{:S(2)}, u32[]{:S(2)}) %collective-permute-start.3) | collective-permute-done | bytes 67616 | tf_op jit(solution)/shard_map/ppermute | solution.py:23
  14.9 0.7 pad_maximum_fusion.2
  15.5 0.7 fusion.28
  16.2 0.0 slice-start
  16.2 0.3 pad_maximum_fusion.1
  16.6 0.0 slice-start.1
  16.6 1.0 fusion.27
  17.6 0.8 slice-done
  18.4 0.2 slice-done.1
  18.6 1.8 %fusion.12 = f32[1024,512]{1,0:T(8,128)S(1)} fusion(bf16[1024,1536]{1,0:T(8,128)(2,1)S(1)} %bitcast.38, bf16[4608,512]{1,0:T(8,128)(2,1)S(1)} %bitcast.47), kind=kOutput, calls=%fused_computation.17 | convolution fusion | flops 1610612736 | bytes 6815744 | tf_op jit(solution)/shard_map/dot_general | solution.py:191
  20.4 1.8 %fusion.14 = f32[1024,512]{1,0:T(8,128)S(1)} fusion(bf16[1024,1536]{1,0:T(8,128)(2,1)S(1)} %bitcast.40, bf16[4608,512]{1,0:T(8,128)(2,1)S(1)} %bitcast.47), kind=kOutput, calls=%fused_computation.19 | convolution fusion | flops 1610612736 | bytes 6815744 | tf_op jit(solution)/shard_map/dot_general | solution.py:191
  22.2 2.5 %fusion.4 = bf16[1024,512]{1,0:T(8,128)(2,1)S(1)} fusion(f32[16,64,512]{2,1,0:T(8,128)S(1)} %copy.7, f32[1024,512]{1,0:T(8,128)S(1)} %fusion.12, f32[1024,512]{1,0:T(8,128)S(1)} %fusion.14, bf16[1024,1536]{1,0:T(8,128)(2,1)S(1)} %bitcast.42, bf16[4608,512]{1,0:T(8,128)(2,1)S(1)} %bitcast.47), kind=kOutput, calls=%fused_computation.9 | convolution fusion | flops 1616379904 | bytes 12058624 | tf_op jit(solution)/shard_map/dot_general | solution.py:191
  24.6 1.9 %fusion.32 = f32[1536,512]{1,0:T(8,128)S(1)} fusion(bf16[1024,1536]{1,0:T(8,128)(2,1)S(1)} %bitcast.43, bf16[1024,512]{1,0:T(8,128)(2,1)S(1)} %fusion.4), kind=kOutput, calls=%fused_computation.42 | convolution fusion | flops 1610612736 | bytes 7340032 | tf_op jit(solution)/shard_map/dot_general | solution.py:197
  26.5 3.5 %fusion.33 = f32[1536,512]{1,0:T(8,128)} fusion(bf16[1024,1536]{1,0:T(8,128)(2,1)S(1)} %bitcast.41, bf16[1024,512]{1,0:T(8,128)(2,1)S(1)} %fusion.4), kind=kOutput, calls=%fused_computation.43 | convolution fusion | flops 1610612736 | bytes 7340032 | tf_op jit(solution)/shard_map/dot_general | solution.py:197
  30.0 0.1 fusion.30
  30.1 1.3 collective-permute-start.4
  31.4 3.5 %fusion.34 = f32[1536,512]{1,0:T(8,128)} fusion(bf16[1024,1536]{1,0:T(8,128)(2,1)S(1)} %bitcast.39, bf16[1024,512]{1,0:T(8,128)(2,1)S(1)} %fusion.4), kind=kOutput, calls=%fused_computation.44 | convolution fusion | flops 1610612736 | bytes 7340032 | tf_op jit(solution)/shard_map/dot_general | solution.py:197
  34.9 0.8 collective-permute-start.5
  35.7 0.6 constant_dynamic-update-slice_fusion.1
  36.3 2.3 %collective-permute-done.5 = bf16[16,1,512]{2,0,1:T(8,128)(2,1)S(1)} collective-permute-done((bf16[16,1,512]{2,0,1:T(8,128)(2,1)S(1)}, bf16[16,1,512]{2,0,1:T(8,128)(2,1)S(1)}, u32[]{:S(2)}, u32[]{:S(2)}) %collective-permute-start.5) | collective-permute-done | bytes 16416 | tf_op jit(solution)/shard_map/ppermute | solution.py:23
  38.7 1.0 copy-done.2
  39.7 0.9 fusion.29
  40.6 4.1 %collective-permute-start.6 = (bf16[1,66,512]{2,0,1:T(2,128)(2,1)}, bf16[1,66,512]{2,0,1:T(2,128)(2,1)}, u32[]{:S(2)}, u32[]{:S(2)}) collective-permute-start(bf16[1,66,512]{2,0,1:T(2,128)(2,1)} %get-tuple-element.18), channel_id=1, source_target_pairs={{0,2},{2,4},{4,6},{6,8},{8,10},{10,12},{12,14},{14,16},{16,18},{18... | collective-permute-start | bytes 202760 | tf_op jit(solution)/shard_map/ppermute | solution.py:20
  44.7 1.5 %collective-permute-start.7 = (bf16[1,66,512]{2,0,1:T(2,128)(2,1)}, bf16[1,66,512]{2,0,1:T(2,128)(2,1)}, u32[]{:S(2)}, u32[]{:S(2)}) collective-permute-start(bf16[1,66,512]{2,0,1:T(2,128)(2,1)} %get-tuple-element.19), channel_id=1, source_target_pairs={{2,0},{4,2},{6,4},{8,6},{10,8},{12,10},{14,12},{16,14},{18,16},{20... | collective-permute-start | bytes 202760 | tf_op jit(solution)/shard_map/ppermute | solution.py:23
  46.2 7.6 %pad_maximum_fusion.refs_0_ = f32[4608,512]{1,0:T(8,128)} fusion(f32[1536,512]{1,0:T(8,128)} %fusion.34, f32[1536,512]{1,0:T(8,128)} %fusion.33, f32[1536,512]{1,0:T(8,128)S(1)} %fusion.32), kind=kLoop, calls=%fused_computation | loop fusion | flops 4718592 | bytes 18874368 | tf_op jit(solution)/shard_map/concatenate | solution.py:195
  53.9 66.2 %shard_map.58 = (f32[288,512]{1,0:T(8,128)S(1)}, f32[288,512]{1,0:T(8,128)S(1)}) custom-call(f32[4608,512]{1,0:T(8,128)} %pad_maximum_fusion.refs_0_, bf16[288,512]{1,0:T(8,128)(2,1)S(1)} %constant_dynamic-slice_fusion.refs_1_), custom_call_target="tpu_custom_call" | custom-call | tf_op jit(solution)/shard_map/pallas_call | solution.py:158
  120.1 0.0 slice-start.3
  120.1 2.1 %maximum_bitcast_fusion = bf16[18,1,66,512]{3,0,2,1:T(8,128)(2,1)S(1)} fusion(bf16[1,66,512]{2,0,1:T(2,128)(2,1)} %collective-permute-done.7, bf16[16,66,512]{2,0,1:T(8,128)(2,1)S(1)} %copy-done.3, bf16[1,66,512]{2,0,1:T(2,128)(2,1)} %collective-permute-done.6), kind=kLoop, calls=%fused_computation.15 | loop fusion | flops 3649536 | bytes 2433024 | tf_op jit(solution)/shard_map/broadcast_in_dim | solution.py:208
  122.2 0.2 pad
  122.4 0.0 copy-start.4
  122.4 0.4 copy.12
  122.8 0.1 slice.92
  122.9 0.2 copy-done.4
  123.1 5.7 %fusion.18 = f32[16,8,9,512]{3,1,2,0:T(8,128)S(1)} fusion(bf16[3,3,512,512]{3,2,1,0:T(8,128)(2,1)S(1)} %bitcast.50, bf16[18,1,7,2,512]{4,2,3,0,1:T(8,128)(2,1)S(1)} %slice.92, bf16[18,1,8,9,512]{4,2,3,0,1:T(8,128)(2,1)S(1)} %copy.12, pred[8,9]{0,1:T(8,128)(4,1)S(1)} %copy-done.4), kind=kOutput, calls=%fused_computation.23 | convolution fusion | flops 5441273856 | bytes 8663112 | tf_op jit(solution)/shard_map/conv_general_dilated | solution.py:207
  128.8 1.4 %copy.13 = f32[16,8,9,512]{3,0,2,1:T(8,128)S(1)} copy(f32[16,8,9,512]{3,1,2,0:T(8,128)S(1)} %fusion.18) | data formatting | bytes 4718592 | tf_op jit(solution)/shard_map/conv_general_dilated | solution.py:207
  130.2 0.8 fusion.2
  131.0 1.5 %copy.14 = bf16[16,64,512]{2,1,0:T(8,128)(2,1)} copy(bf16[16,64,512]{2,0,1:T(8,128)(2,1)S(1)} %fusion.2) | data formatting | bytes 2097152
  132.5 0.8 copy.25
  133.3 0.8 copy.26
  (22 shorter events, 0.1 us)
Async XLA Ops:
  1.7 6.2 %collective-permute-start = (bf16[16,1,512]{2,1,0:T(2,128)(2,1)S(1)}, bf16[16,1,512]{2,1,0:T(2,128)(2,1)S(1)}, u32[]{:S(2)}, u32[]{:S(2)}) collective-permute-start(bf16[16,1,512]{2,1,0:T(2,128)(2,1)S(1)} %get-tuple-element.22), channel_id=1, source_target_pairs={{0,1},{1,0},{2,3},{3,2},{4,5},{5,4},{6,7},{7,6},{8,9},{9,8},{10,11... | collective-permute-start | bytes 49160 | tf_op jit(solution)/shard_map/ppermute | solution.py:20
  4.7 3.9 %collective-permute-start.1 = (bf16[16,1,512]{2,1,0:T(2,128)(2,1)S(1)}, bf16[16,1,512]{2,1,0:T(2,128)(2,1)S(1)}, u32[]{:S(2)}, u32[]{:S(2)}) collective-permute-start(bf16[16,1,512]{2,1,0:T(2,128)(2,1)S(1)} %get-tuple-element.23), channel_id=1, source_target_pairs={{1,0},{0,1},{3,2},{2,3},{5,4},{4,5},{7,6},{6,7},{9,8},{8,9},{11,10... | collective-permute-start | bytes 49160 | tf_op jit(solution)/shard_map/ppermute | solution.py:23
  6.6 2.0 %copy-start = (bf16[16,64,512]{2,1,0:T(8,128)(2,1)S(1)}, bf16[16,64,512]{2,1,0:T(8,128)(2,1)}, u32[]{:S(2)}) copy-start(bf16[16,64,512]{2,1,0:T(8,128)(2,1)} %param.3) | copy-start | bytes 3145732
  8.7 3.8 %collective-permute-start.2 = (bf16[1,66,512]{2,1,0:T(8,128)(2,1)S(1)}, bf16[1,66,512]{2,1,0:T(8,128)(2,1)S(1)}, u32[]{:S(2)}, u32[]{:S(2)}) collective-permute-start(bf16[1,66,512]{2,1,0:T(8,128)(2,1)S(1)} %get-tuple-element.16), channel_id=1, source_target_pairs={{0,2},{2,4},{4,6},{6,8},{8,10},{10,12},{12,14},{14,16},{16,18},{18... | collective-permute-start | bytes 202760 | tf_op jit(solution)/shard_map/ppermute | solution.py:20
  10.0 4.9 %collective-permute-start.3 = (bf16[1,66,512]{2,1,0:T(8,128)(2,1)S(1)}, bf16[1,66,512]{2,1,0:T(8,128)(2,1)S(1)}, u32[]{:S(2)}, u32[]{:S(2)}) collective-permute-start(bf16[1,66,512]{2,1,0:T(8,128)(2,1)S(1)} %get-tuple-element.17), channel_id=1, source_target_pairs={{2,0},{4,2},{6,4},{8,6},{10,8},{12,10},{14,12},{16,14},{18,16},{20... | collective-permute-start | bytes 202760 | tf_op jit(solution)/shard_map/ppermute | solution.py:23
  16.2 2.2 %slice-start = ((s8[4718592]{0:T(1024)(128)(4,1)}), s8[4194304]{0:T(1024)(128)(4,1)S(1)}, s32[]{:S(2)}) async-start(s8[4718592]{0:T(1024)(128)(4,1)} %bitcast.46), calls=%async_computation | async-start | bytes 8388608
  16.6 2.0 %slice-start.1 = ((s8[4718592]{0:T(1024)(128)(4,1)}), s8[524288]{0:T(1024)(128)(4,1)S(1)}, s32[]{:S(2)}) async-start(s8[4718592]{0:T(1024)(128)(4,1)} %bitcast.46), calls=%async_computation.1 | async-start | bytes 1048576
  30.1 5.6 %collective-permute-start.4 = (bf16[16,1,512]{2,0,1:T(8,128)(2,1)S(1)}, bf16[16,1,512]{2,0,1:T(8,128)(2,1)S(1)}, u32[]{:S(2)}, u32[]{:S(2)}) collective-permute-start(bf16[16,1,512]{2,0,1:T(8,128)(2,1)S(1)} %copy.19), channel_id=1, source_target_pairs={{0,1},{1,0},{2,3},{3,2},{4,5},{5,4},{6,7},{7,6},{8,9},{9,8},{10,11... | collective-permute-start | bytes 49160 | tf_op jit(solution)/shard_map/ppermute | solution.py:20
  34.9 3.7 %collective-permute-start.5 = (bf16[16,1,512]{2,0,1:T(8,128)(2,1)S(1)}, bf16[16,1,512]{2,0,1:T(8,128)(2,1)S(1)}, u32[]{:S(2)}, u32[]{:S(2)}) collective-permute-start(bf16[16,1,512]{2,0,1:T(8,128)(2,1)S(1)} %copy.20), channel_id=1, source_target_pairs={{1,0},{0,1},{3,2},{2,3},{5,4},{4,5},{7,6},{6,7},{9,8},{8,9},{11,10... | collective-permute-start | bytes 49160 | tf_op jit(solution)/shard_map/ppermute | solution.py:23
  38.7 1.0 copy-start.2
  40.6 79.5 %collective-permute-start.6 = (bf16[1,66,512]{2,0,1:T(2,128)(2,1)}, bf16[1,66,512]{2,0,1:T(2,128)(2,1)}, u32[]{:S(2)}, u32[]{:S(2)}) collective-permute-start(bf16[1,66,512]{2,0,1:T(2,128)(2,1)} %get-tuple-element.18), channel_id=1, source_target_pairs={{0,2},{2,4},{4,6},{6,8},{8,10},{10,12},{12,14},{14,16},{16,18},{18... | collective-permute-start | bytes 202760 | tf_op jit(solution)/shard_map/ppermute | solution.py:20
  44.7 75.4 %collective-permute-start.7 = (bf16[1,66,512]{2,0,1:T(2,128)(2,1)}, bf16[1,66,512]{2,0,1:T(2,128)(2,1)}, u32[]{:S(2)}, u32[]{:S(2)}) collective-permute-start(bf16[1,66,512]{2,0,1:T(2,128)(2,1)} %get-tuple-element.19), channel_id=1, source_target_pairs={{2,0},{4,2},{6,4},{8,6},{10,8},{12,10},{14,12},{16,14},{18,16},{20... | collective-permute-start | bytes 202760 | tf_op jit(solution)/shard_map/ppermute | solution.py:23
  53.9 66.3 %copy-start.3 = (bf16[16,66,512]{2,0,1:T(8,128)(2,1)S(1)}, bf16[16,66,512]{2,0,1:T(8,128)(2,1)}, u32[]{:S(2)}) copy-start(bf16[16,66,512]{2,0,1:T(8,128)(2,1)} %copy-done.2) | copy-start | bytes 3244036
  53.9 69.0 %slice-start.2 = ((s8[4718592]{0:T(1024)(128)(4,1)}), s8[4194304]{0:T(1024)(128)(4,1)S(1)}, s32[]{:S(2)}) async-start(s8[4718592]{0:T(1024)(128)(4,1)} %bitcast.48), calls=%async_computation.2 | async-start | bytes 8388608
  120.1 2.8 %slice-start.3 = ((s8[4718592]{0:T(1024)(128)(4,1)}), s8[524288]{0:T(1024)(128)(4,1)S(1)}, s32[]{:S(2)}) async-start(s8[4718592]{0:T(1024)(128)(4,1)} %bitcast.48), calls=%async_computation.3 | async-start | bytes 1048576
  122.4 0.7 copy-start.4
  128.8 1.4 %copy-start.1 = (bf16[16,64,512]{2,1,0:T(8,128)(2,1)S(1)}, bf16[16,64,512]{2,1,0:T(8,128)(2,1)}, u32[]{:S(2)}) copy-start(bf16[16,64,512]{2,1,0:T(8,128)(2,1)} %param.4) | copy-start | bytes 3145732

commit v2 on v1

--- a/solution.py
+++ b/solution.py
@@ -39,9 +39,21 @@
 
 
 def reduce_kernel(n_lat, n_lon, count, *refs):
-    grad, own, direction, perturbed, acc, send, recv, beside, squares = refs[:9]
-    send_sem, recv_sem, lon_send, lon_recv, sq_send, sq_recv = refs[9:]
+    parts, own, direction, perturbed = refs[:3], refs[3], refs[4], refs[5]
+    grad, acc, send, recv, beside, squares = refs[6:12]
+    send_sem, recv_sem, lon_send, lon_recv, sq_send, sq_recv, load_sem = refs[12:]
     rows, channels = own.shape
+    pieces = send_sem.shape[1]
+    width = channels // pieces
+    part_rows = parts[0].shape[0]
+    loads = [
+        pltpu.make_async_copy(
+            part, grad.at[pl.ds(a * part_rows, part_rows)], load_sem.at[a]
+        )
+        for a, part in enumerate(parts)
+    ]
+    for load in loads:
+        load.start()
     lat = lax.axis_index("lat")
     lon = lax.axis_index("lon")
     stages = n_lat.bit_length() - 1
@@ -57,6 +69,8 @@
             barrier, inc=1, device_id={"lon": lax.rem(lon + k, n_lon)}, device_id_type=MESH
         )
     pl.semaphore_wait(barrier, n_lat + n_lon - 2)
+    for load in loads:
+        load.wait()
 
     base = [0]
     for s in range(stages):
@@ -69,48 +83,56 @@
                 block = block + 2**s * (1 - 2 * bit[s])
         return pl.ds(pl.multiple_of(block * rows, 16), rows)
 
-    def copy(s, slot):
+    def columns(piece):
+        return pl.ds(piece * width, width)
+
+    def copy(s, slot, piece):
         k = base[s] + slot
         return pltpu.make_async_remote_copy(
-            src_ref=send.at[k],
-            dst_ref=recv.at[k],
-            send_sem=send_sem.at[k],
-            recv_sem=recv_sem.at[k],
+            src_ref=send.at[k, :, columns(piece)],
+            dst_ref=recv.at[k, :, columns(piece)],
+            send_sem=send_sem.at[k, piece],
+            recv_sem=recv_sem.at[k, piece],
             device_id={"lat": lat + 2**s * (1 - 2 * bit[s])},
             device_id_type=MESH,
         )
 
+    def lon_copy(k, source, piece):
+        return pltpu.make_async_remote_copy(
+            src_ref=beside.at[source, :, columns(piece)],
+            dst_ref=beside.at[source, :, columns(piece)],
+            send_sem=lon_send.at[k, piece],
+            recv_sem=lon_recv.at[source, piece],
+            device_id={"lon": lax.rem(lon + k, n_lon)},
+            device_id_type=MESH,
+        )
+
+    def pass_on(s, slot, piece, value):
+        send[base[s] + slot, :, columns(piece)] = value.astype(jnp.bfloat16)
+        copy(s, slot, piece).start()
+
     for slot in slots_in_order(stages - 1):
-        send[base[0] + slot] = grad[rows_of(2 * slot + 1), :].astype(jnp.bfloat16)
-        copy(0, slot).start()
+        for piece in range(pieces):
+            pass_on(0, slot, piece, grad[rows_of(2 * slot + 1), columns(piece)])
     for s in range(stages):
         for slot in slots_in_order(stages - 1 - s):
-            copy(s, slot).wait_recv()
-            got = recv[base[s] + slot].astype(jnp.float32)
-            r = slot << (s + 1)
-            value = got + (grad[rows_of(r), :] if s == 0 else acc[r >> 1])
-            if s + 1 == stages:
-                beside[lon] = value.astype(jnp.bfloat16)
-            elif slot % 2:
-                send[base[s + 1] + slot // 2] = value.astype(jnp.bfloat16)
-                copy(s + 1, slot // 2).start()
-            else:
-                acc[r >> 1] = value
-
-    def lon_copy(k, source):
-        return pltpu.make_async_remote_copy(
-            src_ref=beside.at[source],
-            dst_ref=beside.at[source],
-            send_sem=lon_send.at[k],
-            recv_sem=lon_recv.at[source],
-            device_id={"lon": lax.rem(lon + k, n_lon)},
-            device_id_type=MESH,
-        )
-
-    for k in range(1, n_lon):
-        lon_copy(k, lon).start()
-    for k in range(1, n_lon):
-        lon_copy(k, lax.rem(lon + k, n_lon)).wait_recv()
+            for piece in range(pieces):
+                copy(s, slot, piece).wait_recv()
+                cols = columns(piece)
+                got = recv[base[s] + slot, :, cols].astype(jnp.float32)
+                r = slot << (s + 1)
+                value = got + (grad[rows_of(r), cols] if s == 0 else acc[r >> 1, :, cols])
+                if s + 1 == stages:
+                    beside[lon, :, cols] = value.astype(jnp.bfloat16)
+                    for k in range(1, n_lon):
+                        lon_copy(k, lon, piece).start()
+                elif slot % 2:
+                    pass_on(s + 1, slot // 2, piece, value)
+                else:
+                    acc[r >> 1, :, cols] = value
+    for piece in range(pieces):
+        for k in range(1, n_lon):
+            lon_copy(k, lax.rem(lon + k, n_lon), piece).wait_recv()
     summed = beside[0].astype(jnp.float32)
     for k in range(1, n_lon):
         summed = summed + beside[k].astype(jnp.float32)
@@ -141,16 +163,17 @@
     direction[...] = scaled
     perturbed[...] = own[...].astype(jnp.float32) + 0.05 / count**0.5 * scaled
 
-    for s in range(stages):
-        for slot in range(n_lat >> (s + 1)):
-            copy(s, slot).wait_send()
-    for k in range(1, n_lon):
-        lon_copy(k, lon).wait_send()
+    for piece in range(pieces):
+        for s in range(stages):
+            for slot in range(n_lat >> (s + 1)):
+                copy(s, slot, piece).wait_send()
+        for k in range(1, n_lon):
+            lon_copy(k, lon, piece).wait_send()
     for k in range(1, n_lat):
         square_copy(k, lat).wait_send()
 
 
-def reduce_and_scale(grad, own, count):
+def reduce_and_scale(grads, own, count, pieces=2):
     n_lat, n_lon = lax.axis_size("lat"), lax.axis_size("lon")
     rows, channels = own.shape
     block = jax.ShapeDtypeStruct((rows, channels), jnp.float32)
@@ -158,25 +181,27 @@
     return pl.pallas_call(
         functools.partial(reduce_kernel, n_lat, n_lon, count),
         out_shape=(block, block),
-        in_specs=[vmem, vmem],
+        in_specs=[pl.BlockSpec(memory_space=pl.ANY)] * 3 + [vmem],
         out_specs=(vmem, vmem),
         scratch_shapes=[
+            pltpu.VMEM((rows * n_lat, channels), jnp.float32),
             pltpu.VMEM((n_lat // 2, rows, channels), jnp.float32),
             pltpu.VMEM((n_lat - 1, rows, channels), jnp.bfloat16),
             pltpu.VMEM((n_lat - 1, rows, channels), jnp.bfloat16),
             pltpu.VMEM((n_lon, rows, channels), jnp.bfloat16),
             pltpu.VMEM((n_lat, 8, 128), jnp.float32),
-            pltpu.SemaphoreType.DMA((n_lat - 1,)),
-            pltpu.SemaphoreType.DMA((n_lat - 1,)),
-            pltpu.SemaphoreType.DMA((n_lon,)),
-            pltpu.SemaphoreType.DMA((n_lon,)),
+            pltpu.SemaphoreType.DMA((n_lat - 1, pieces)),
+            pltpu.SemaphoreType.DMA((n_lat - 1, pieces)),
+            pltpu.SemaphoreType.DMA((n_lon, pieces)),
+            pltpu.SemaphoreType.DMA((n_lon, pieces)),
             pltpu.SemaphoreType.DMA((n_lat,)),
             pltpu.SemaphoreType.DMA((n_lat,)),
+            pltpu.SemaphoreType.DMA((3,)),
         ],
         compiler_params=pltpu.CompilerParams(
             collective_id=0, has_side_effects=True, vmem_limit_bytes=48 * 2**20
         ),
-    )(grad, own)
+    )(*grads, own)
 
 
 def shards(features, upstream, kernel):
@@ -192,15 +217,10 @@
         for a in range(3)
     )
     slope = gated(upstream.reshape(-1, channels), z).astype(jnp.bfloat16)
-    local_grad = jnp.concatenate(
-        [
-            lax.dot_general(
-                view, slope, (((0,), (0,)), ((), ())), preferred_element_type=jnp.float32
-            )
-            for view in views
-        ],
-        axis=0,
-    )
+    local_grads = [
+        lax.dot_general(view, slope, (((0,), (0,)), ((), ())), preferred_element_type=jnp.float32)
+        for view in views
+    ]
     slope = slope.reshape(height, breadth, channels)
     slope_cols = padded_2(slope, (("lon", 1),), 1, True)
     padded_slope = padded_2(slope_cols, (("lat", 0),), 1, False)
@@ -217,7 +237,7 @@
     block_rows = kernel.shape[0] // lax.axis_size("lat")
     start = lax.axis_index("lat") * block_rows
     own_kernel = lax.dynamic_slice_in_dim(kernel, start, block_rows, 0)
-    direction, perturbed = reduce_and_scale(local_grad, own_kernel, count)
+    direction, perturbed = reduce_and_scale(local_grads, own_kernel, count)
     return (input_grad, direction, perturbed)
 
 

time: 134 us -> 116 us (0.87)
  other arithmetic: 13.4 us -> 4.8 us
  Pallas kernels: 66.2 us -> 60.8 us
  waiting for transfers between devices: 5.53 us -> 3.11 us
  local copies, waits for them, and re-layouts: 13.9 us -> 12.2 us
    concatenate x1 -> x0, other arithmetic: 7.63 us -> none  [shards(): jnp.concatenate([lax.dot_general(view, slope, (((0,), (0,)), ((), ())), p...]
    pallas_call x1, Pallas kernels: 66.2 us -> 60.8 us  [reduce_and_scale(): pl.pallas_call(functools.partial(reduce_kernel, n_lat, n_lon, count), out...]
    ppermute x4, waiting for transfers between devices: 5.52 us -> 2.36 us  [padded_2(): lax.ppermute(lax.slice_in_dim(block, 0, width, axis=dim), axis, backward)]
    ppermute x4, starting transfers between devices: 3.85 us -> 6.41 us  [padded_2(): lax.ppermute(lax.slice_in_dim(block, 0, width, axis=dim), axis, backward)]
    ppermute x4, starting transfers between devices: 9.75 us -> 7.44 us  [padded_2(): lax.ppermute(lax.slice_in_dim(block, block.shape[dim] - width, None, axis...]
    unnamed x25 -> x21, local copies, waits for them, and re-layouts: 5.96 us -> 5.16 us
  transfers between devices with their start and end apart: 8 -> 8, of which waited for: 3 -> 2; matrix products, arithmetic and copies ran while one was open for 12% -> 10% of each run, Pallas kernels for 49% -> 52%
where the time goes in v2:
time: 116 us
  Pallas kernels  60.8 us (52%)
  matrix products  20.5 us (18%)
  starting transfers between devices  13.9 us (12%)
  local copies, waits for them, and re-layouts  12.2 us (11%)
  other arithmetic  4.8 us (4%)
  waiting for transfers between devices  3.11 us (3%)
    pallas_call x1, Pallas kernels, reduce_and_scale(): pl.pallas_call(functools.partial(reduce_kernel, n_lat, n_lon, count), out...  60.8 us
    dot_general x3, matrix products, shards(): lax.dot_general(view, slope, (((0,), (0,)), ((), ())), preferred_element_...  8.84 us
    ppermute x4, starting transfers between devices, padded_2(): lax.ppermute(lax.slice_in_dim(block, block.shape[dim] - width, None, axis...  7.44 us
    ppermute x4, starting transfers between devices, padded_2(): lax.ppermute(lax.slice_in_dim(block, 0, width, axis=dim), axis, backward)  6.41 us
    dot_general x3, matrix products, shards(): jnp.dot(views[a], kernel[a * wide:(a + 1) * wide], preferred_element_type...  5.97 us
    conv_general_dilated x1, matrix products, shards(): lax.conv_general_dilated(padded_slope[None], kernel.reshape(3, 3, channel...  5.68 us
    unnamed x21, local copies, waits for them, and re-layouts  5.16 us
    convert_element_type x2, other arithmetic, shards(): input_grad = (upstream.astype(jnp.float32) + back).astype(jnp.bfloat16)  2.66 us
  transfers between devices with their start and end apart: 8, of which 2 were waited for; matrix products, arithmetic and copies ran while one was open for 10% of the time, Pallas kernels for 52%

profile of v2, /device:TPU:0, one launch (start us, length us, event | category | flops | bytes accessed | tf_op | source)
XLA Modules:
  0.0 116.2 jit_solution(1861452669232874856)
XLA Ops:
  0.6 1.0 fusion.31
  1.7 3.0 %collective-permute-start.1 = (bf16[16,1,512]{2,1,0:T(2,128)(2,1)S(1)}, bf16[16,1,512]{2,1,0:T(2,128)(2,1)S(1)}, u32[]{:S(2)}, u32[]{:S(2)}) collective-permute-start(bf16[16,1,512]{2,1,0:T(2,128)(2,1)S(1)} %get-tuple-element.23), channel_id=1, source_target_pairs={{1,0},{0,1},{3,2},{2,3},{5,4},{4,5},{7,6},{6,7},{9,8},{8,9},{11,10... | collective-permute-start | bytes 49160 | tf_op jit(solution)/shard_map/ppermute | solution.py:23
  4.7 0.1 collective-permute-start
  4.8 1.8 %copy_convert_fusion = f32[16,64,512]{2,0,1:T(8,128)S(1)} fusion(bf16[16,64,512]{2,1,0:T(8,128)(2,1)} %param.4), kind=kLoop, calls=%fused_computation.24 | loop fusion | flops 524288 | bytes 3145728 | tf_op jit(solution)/shard_map/convert_element_type | solution.py:235
  6.6 0.0 copy-start
  6.6 1.2 %copy.7 = f32[16,64,512]{2,1,0:T(8,128)S(1)} copy(f32[16,64,512]{2,0,1:T(8,128)S(1)} %copy_convert_fusion) | data formatting | bytes 4194304 | tf_op jit(solution)/shard_map/convert_element_type | solution.py:235
  7.9 0.7 collective-permute-done
  8.7 1.3 %collective-permute-start.3 = (bf16[1,66,512]{2,1,0:T(8,128)(2,1)S(1)}, bf16[1,66,512]{2,1,0:T(8,128)(2,1)S(1)}, u32[]{:S(2)}, u32[]{:S(2)}) collective-permute-start(bf16[1,66,512]{2,1,0:T(8,128)(2,1)S(1)} %get-tuple-element.17), channel_id=1, source_target_pairs={{2,0},{4,2},{6,4},{8,6},{10,8},{12,10},{14,12},{16,14},{18,16},{20... | collective-permute-start | bytes 202760 | tf_op jit(solution)/shard_map/ppermute | solution.py:23
  10.0 3.0 %collective-permute-start.2 = (bf16[1,66,512]{2,1,0:T(8,128)(2,1)S(1)}, bf16[1,66,512]{2,1,0:T(8,128)(2,1)S(1)}, u32[]{:S(2)}, u32[]{:S(2)}) collective-permute-start(bf16[1,66,512]{2,1,0:T(8,128)(2,1)S(1)} %get-tuple-element.16), channel_id=1, source_target_pairs={{0,2},{2,4},{4,6},{6,8},{8,10},{10,12},{12,14},{14,16},{16,18},{18... | collective-permute-start | bytes 202760 | tf_op jit(solution)/shard_map/ppermute | solution.py:20
  13.0 1.0 constant_dynamic-slice_fusion.refs_3_
  14.0 0.0 collective-permute-done.3
  14.0 0.6 pad_maximum_fusion.1
  14.7 0.7 fusion.28
  15.4 0.0 slice-start
  15.4 0.3 pad_maximum_fusion
  15.7 0.0 slice-start.1
  15.7 0.8 fusion.27
  16.5 1.0 slice-done
  17.5 0.2 slice-done.1
  17.7 1.8 %fusion.12 = f32[1024,512]{1,0:T(8,128)S(1)} fusion(bf16[1024,1536]{1,0:T(8,128)(2,1)S(1)} %bitcast.38, bf16[4608,512]{1,0:T(8,128)(2,1)S(1)} %bitcast.47), kind=kOutput, calls=%fused_computation.16 | convolution fusion | flops 1610612736 | bytes 6815744 | tf_op jit(solution)/shard_map/dot_general | solution.py:216
  19.5 1.8 %fusion.14 = f32[1024,512]{1,0:T(8,128)S(1)} fusion(bf16[1024,1536]{1,0:T(8,128)(2,1)S(1)} %bitcast.40, bf16[4608,512]{1,0:T(8,128)(2,1)S(1)} %bitcast.47), kind=kOutput, calls=%fused_computation.18 | convolution fusion | flops 1610612736 | bytes 6815744 | tf_op jit(solution)/shard_map/dot_general | solution.py:216
  21.3 2.4 %fusion.4 = bf16[1024,512]{1,0:T(8,128)(2,1)S(1)} fusion(f32[16,64,512]{2,1,0:T(8,128)S(1)} %copy.7, f32[1024,512]{1,0:T(8,128)S(1)} %fusion.12, f32[1024,512]{1,0:T(8,128)S(1)} %fusion.14, bf16[1024,1536]{1,0:T(8,128)(2,1)S(1)} %bitcast.42, bf16[4608,512]{1,0:T(8,128)(2,1)S(1)} %bitcast.47), kind=kOutput, calls=%fused_computation.8 | convolution fusion | flops 1616379904 | bytes 12058624 | tf_op jit(solution)/shard_map/dot_general | solution.py:216
  23.7 1.9 %fusion.32.refs_0_ = f32[1536,512]{1,0:T(8,128)S(1)} fusion(bf16[1024,1536]{1,0:T(8,128)(2,1)S(1)} %bitcast.43, bf16[1024,512]{1,0:T(8,128)(2,1)S(1)} %fusion.4), kind=kOutput, calls=%fused_computation.41 | convolution fusion | flops 1610612736 | bytes 7340032 | tf_op jit(solution)/shard_map/dot_general | solution.py:221
  25.6 0.1 fusion.30
  25.7 1.3 %collective-permute-start.4 = (bf16[16,1,512]{2,0,1:T(8,128)(2,1)S(1)}, bf16[16,1,512]{2,0,1:T(8,128)(2,1)S(1)}, u32[]{:S(2)}, u32[]{:S(2)}) collective-permute-start(bf16[16,1,512]{2,0,1:T(8,128)(2,1)S(1)} %copy.19), channel_id=1, source_target_pairs={{0,1},{1,0},{2,3},{3,2},{4,5},{5,4},{6,7},{7,6},{8,9},{9,8},{10,11... | collective-permute-start | bytes 49160 | tf_op jit(solution)/shard_map/ppermute | solution.py:20
  27.0 3.5 %fusion.33.refs_1_ = f32[1536,512]{1,0:T(8,128)} fusion(bf16[1024,1536]{1,0:T(8,128)(2,1)S(1)} %bitcast.41, bf16[1024,512]{1,0:T(8,128)(2,1)S(1)} %fusion.4), kind=kOutput, calls=%fused_computation.42 | convolution fusion | flops 1610612736 | bytes 7340032 | tf_op jit(solution)/shard_map/dot_general | solution.py:221
  30.4 0.8 collective-permute-start.5
  31.3 0.6 constant_dynamic-update-slice_fusion.1
  31.8 2.4 %collective-permute-done.5 = bf16[16,1,512]{2,0,1:T(8,128)(2,1)S(1)} collective-permute-done((bf16[16,1,512]{2,0,1:T(8,128)(2,1)S(1)}, bf16[16,1,512]{2,0,1:T(8,128)(2,1)S(1)}, u32[]{:S(2)}, u32[]{:S(2)}) %collective-permute-start.5) | collective-permute-done | bytes 16416 | tf_op jit(solution)/shard_map/ppermute | solution.py:23
  34.2 0.2 fusion.29
  34.4 1.3 %collective-permute-start.7 = (bf16[1,66,512]{2,0,1:T(2,128)(2,1)S(1)}, bf16[1,66,512]{2,0,1:T(2,128)(2,1)S(1)}, u32[]{:S(2)}, u32[]{:S(2)}) collective-permute-start(bf16[1,66,512]{2,0,1:T(2,128)(2,1)S(1)} %get-tuple-element.19), channel_id=1, source_target_pairs={{2,0},{4,2},{6,4},{8,6},{10,8},{12,10},{14,12},{16,14},{18,16},{20... | collective-permute-start | bytes 202760 | tf_op jit(solution)/shard_map/ppermute | solution.py:23
  35.7 3.0 %collective-permute-start.6 = (bf16[1,66,512]{2,0,1:T(2,128)(2,1)S(1)}, bf16[1,66,512]{2,0,1:T(2,128)(2,1)S(1)}, u32[]{:S(2)}, u32[]{:S(2)}) collective-permute-start(bf16[1,66,512]{2,0,1:T(2,128)(2,1)S(1)} %get-tuple-element.18), channel_id=1, source_target_pairs={{0,2},{2,4},{4,6},{6,8},{8,10},{10,12},{12,14},{14,16},{16,18},{18... | collective-permute-start | bytes 202760 | tf_op jit(solution)/shard_map/ppermute | solution.py:20
  38.8 3.5 %fusion.34.refs_2_ = f32[1536,512]{1,0:T(8,128)} fusion(bf16[1024,1536]{1,0:T(8,128)(2,1)S(1)} %bitcast.39, bf16[1024,512]{1,0:T(8,128)(2,1)S(1)} %fusion.4), kind=kOutput, calls=%fused_computation.43 | convolution fusion | flops 1610612736 | bytes 7340032 | tf_op jit(solution)/shard_map/dot_general | solution.py:221
  42.3 60.8 %shard_map.58 = (f32[288,512]{1,0:T(8,128)S(1)}, f32[288,512]{1,0:T(8,128)S(1)}) custom-call(f32[1536,512]{1,0:T(8,128)S(1)} %fusion.32.refs_0_, f32[1536,512]{1,0:T(8,128)} %fusion.33.refs_1_, f32[1536,512]{1,0:T(8,128)} %fusion.34.refs_2_, bf16[288,512]{1,0:T(8,128)(2,1)S(1)} %constant_dynamic-slice_fusion.refs_3_), custom_call_target="tpu_custom_call" | custom-call | tf_op jit(solution)/shard_map/pallas_call | solution.py:181
  103.1 0.0 slice-start.3
  103.1 1.1 maximum_bitcast_fusion
  104.2 0.2 pad
  104.4 0.0 copy-start.2
  104.4 0.4 copy.12
  104.8 0.1 slice.92
  104.9 0.2 copy-done.2
  105.1 5.7 %fusion.18 = f32[16,8,9,512]{3,1,2,0:T(8,128)S(1)} fusion(bf16[3,3,512,512]{3,2,1,0:T(8,128)(2,1)S(1)} %bitcast.50, bf16[18,1,7,2,512]{4,2,3,0,1:T(8,128)(2,1)S(1)} %slice.92, bf16[18,1,8,9,512]{4,2,3,0,1:T(8,128)(2,1)S(1)} %copy.12, pred[8,9]{0,1:T(8,128)(4,1)S(1)} %copy-done.2), kind=kOutput, calls=%fused_computation.22 | convolution fusion | flops 5441273856 | bytes 8663112 | tf_op jit(solution)/shard_map/conv_general_dilated | solution.py:227
  110.8 0.0 copy-start.1
  110.8 1.4 %copy.13 = f32[16,8,9,512]{3,0,2,1:T(8,128)S(1)} copy(f32[16,8,9,512]{3,1,2,0:T(8,128)S(1)} %fusion.18) | data formatting | bytes 4718592 | tf_op jit(solution)/shard_map/conv_general_dilated | solution.py:227
  112.2 0.8 fusion.2
  113.0 1.5 %copy.14 = bf16[16,64,512]{2,1,0:T(8,128)(2,1)} copy(bf16[16,64,512]{2,0,1:T(8,128)(2,1)S(1)} %fusion.2) | data formatting | bytes 2097152
  114.5 0.8 copy.25
  115.4 0.8 copy.26
  (17 shorter events, 0.1 us)
Async XLA Ops:
  1.7 6.2 %collective-permute-start.1 = (bf16[16,1,512]{2,1,0:T(2,128)(2,1)S(1)}, bf16[16,1,512]{2,1,0:T(2,128)(2,1)S(1)}, u32[]{:S(2)}, u32[]{:S(2)}) collective-permute-start(bf16[16,1,512]{2,1,0:T(2,128)(2,1)S(1)} %get-tuple-element.23), channel_id=1, source_target_pairs={{1,0},{0,1},{3,2},{2,3},{5,4},{4,5},{7,6},{6,7},{9,8},{8,9},{11,10... | collective-permute-start | bytes 49160 | tf_op jit(solution)/shard_map/ppermute | solution.py:23
  4.7 3.9 %collective-permute-start = (bf16[16,1,512]{2,1,0:T(2,128)(2,1)S(1)}, bf16[16,1,512]{2,1,0:T(2,128)(2,1)S(1)}, u32[]{:S(2)}, u32[]{:S(2)}) collective-permute-start(bf16[16,1,512]{2,1,0:T(2,128)(2,1)S(1)} %get-tuple-element.22), channel_id=1, source_target_pairs={{0,1},{1,0},{2,3},{3,2},{4,5},{5,4},{6,7},{7,6},{8,9},{9,8},{10,11... | collective-permute-start | bytes 49160 | tf_op jit(solution)/shard_map/ppermute | solution.py:20
  6.6 2.0 %copy-start = (bf16[16,64,512]{2,1,0:T(8,128)(2,1)S(1)}, bf16[16,64,512]{2,1,0:T(8,128)(2,1)}, u32[]{:S(2)}) copy-start(bf16[16,64,512]{2,1,0:T(8,128)(2,1)} %param.3) | copy-start | bytes 3145732
  8.7 5.3 %collective-permute-start.3 = (bf16[1,66,512]{2,1,0:T(8,128)(2,1)S(1)}, bf16[1,66,512]{2,1,0:T(8,128)(2,1)S(1)}, u32[]{:S(2)}, u32[]{:S(2)}) collective-permute-start(bf16[1,66,512]{2,1,0:T(8,128)(2,1)S(1)} %get-tuple-element.17), channel_id=1, source_target_pairs={{2,0},{4,2},{6,4},{8,6},{10,8},{12,10},{14,12},{16,14},{18,16},{20... | collective-permute-start | bytes 202760 | tf_op jit(solution)/shard_map/ppermute | solution.py:23
  10.0 4.0 %collective-permute-start.2 = (bf16[1,66,512]{2,1,0:T(8,128)(2,1)S(1)}, bf16[1,66,512]{2,1,0:T(8,128)(2,1)S(1)}, u32[]{:S(2)}, u32[]{:S(2)}) collective-permute-start(bf16[1,66,512]{2,1,0:T(8,128)(2,1)S(1)} %get-tuple-element.16), channel_id=1, source_target_pairs={{0,2},{2,4},{4,6},{6,8},{8,10},{10,12},{12,14},{14,16},{16,18},{18... | collective-permute-start | bytes 202760 | tf_op jit(solution)/shard_map/ppermute | solution.py:20
  15.4 2.2 %slice-start = ((s8[4718592]{0:T(1024)(128)(4,1)}), s8[4194304]{0:T(1024)(128)(4,1)S(1)}, s32[]{:S(2)}) async-start(s8[4718592]{0:T(1024)(128)(4,1)} %bitcast.46), calls=%async_computation | async-start | bytes 8388608
  15.7 2.0 %slice-start.1 = ((s8[4718592]{0:T(1024)(128)(4,1)}), s8[524288]{0:T(1024)(128)(4,1)S(1)}, s32[]{:S(2)}) async-start(s8[4718592]{0:T(1024)(128)(4,1)} %bitcast.46), calls=%async_computation.1 | async-start | bytes 1048576
  25.7 5.6 %collective-permute-start.4 = (bf16[16,1,512]{2,0,1:T(8,128)(2,1)S(1)}, bf16[16,1,512]{2,0,1:T(8,128)(2,1)S(1)}, u32[]{:S(2)}, u32[]{:S(2)}) collective-permute-start(bf16[16,1,512]{2,0,1:T(8,128)(2,1)S(1)} %copy.19), channel_id=1, source_target_pairs={{0,1},{1,0},{2,3},{3,2},{4,5},{5,4},{6,7},{7,6},{8,9},{9,8},{10,11... | collective-permute-start | bytes 49160 | tf_op jit(solution)/shard_map/ppermute | solution.py:20
  30.4 3.7 %collective-permute-start.5 = (bf16[16,1,512]{2,0,1:T(8,128)(2,1)S(1)}, bf16[16,1,512]{2,0,1:T(8,128)(2,1)S(1)}, u32[]{:S(2)}, u32[]{:S(2)}) collective-permute-start(bf16[16,1,512]{2,0,1:T(8,128)(2,1)S(1)} %copy.20), channel_id=1, source_target_pairs={{1,0},{0,1},{3,2},{2,3},{5,4},{4,5},{7,6},{6,7},{9,8},{8,9},{11,10... | collective-permute-start | bytes 49160 | tf_op jit(solution)/shard_map/ppermute | solution.py:23
  34.4 68.7 %collective-permute-start.7 = (bf16[1,66,512]{2,0,1:T(2,128)(2,1)S(1)}, bf16[1,66,512]{2,0,1:T(2,128)(2,1)S(1)}, u32[]{:S(2)}, u32[]{:S(2)}) collective-permute-start(bf16[1,66,512]{2,0,1:T(2,128)(2,1)S(1)} %get-tuple-element.19), channel_id=1, source_target_pairs={{2,0},{4,2},{6,4},{8,6},{10,8},{12,10},{14,12},{16,14},{18,16},{20... | collective-permute-start | bytes 202760 | tf_op jit(solution)/shard_map/ppermute | solution.py:23
  35.7 67.4 %collective-permute-start.6 = (bf16[1,66,512]{2,0,1:T(2,128)(2,1)S(1)}, bf16[1,66,512]{2,0,1:T(2,128)(2,1)S(1)}, u32[]{:S(2)}, u32[]{:S(2)}) collective-permute-start(bf16[1,66,512]{2,0,1:T(2,128)(2,1)S(1)} %get-tuple-element.18), channel_id=1, source_target_pairs={{0,2},{2,4},{4,6},{6,8},{8,10},{10,12},{12,14},{14,16},{16,18},{18... | collective-permute-start | bytes 202760 | tf_op jit(solution)/shard_map/ppermute | solution.py:20
  42.3 62.6 %slice-start.2 = ((s8[4718592]{0:T(1024)(128)(4,1)}), s8[4194304]{0:T(1024)(128)(4,1)S(1)}, s32[]{:S(2)}) async-start(s8[4718592]{0:T(1024)(128)(4,1)} %bitcast.48), calls=%async_computation.2 | async-start | bytes 8388608
  103.1 1.8 %slice-start.3 = ((s8[4718592]{0:T(1024)(128)(4,1)}), s8[524288]{0:T(1024)(128)(4,1)S(1)}, s32[]{:S(2)}) async-start(s8[4718592]{0:T(1024)(128)(4,1)} %bitcast.48), calls=%async_computation.3 | async-start | bytes 1048576
  104.4 0.7 copy-start.2
  110.8 1.4 %copy-start.1 = (bf16[16,64,512]{2,1,0:T(8,128)(2,1)S(1)}, bf16[16,64,512]{2,1,0:T(8,128)(2,1)}, u32[]{:S(2)}) copy-start(bf16[16,64,512]{2,1,0:T(8,128)(2,1)} %param.4) | copy-start | bytes 3145732
